TPU v7x, 32 devices: a whole 2x2x4 slice. The times are simulated.
32 devices in a mesh: grp: 4 (over y, x), smp: 8 (over z, core).
Axes of the slice: x: 2, y: 2, z: 4, core: 2. Of those that a mesh axis runs over, the one named last changes fastest.
Arguments:
- spins_packed: int32 [32, 8192], P(None, 'smp'), may hold values from -2147483648 to 2147483646
- weight: bfloat16 [1024, 8192], P(None, 'grp'), may hold values from -0.1875 to 0.1875
- hidden_bias: float32 [8192], P('grp'), may hold values from -1.5 to 1.5
- force_w: float32 [1024, 8192], P('smp', 'grp'), may hold values from -6 to 6
- force_b: float32 [8192], P('grp'), may hold values from -6 to 6
Outputs:
- update_w: float32 [1024, 8192], P('smp', 'grp')
- update_b: float32 [8192], P('grp')
All inputs are finite; a program needn't handle non-finite values.
Results may differ from a plain program's by a relative error of at most 0.0003.
Values sent between devices are 32-bit elements; how exact they have to be, the bound alone decides.
A program may use at most 64 MiB of HBM per device.

v0:
```python
import functools

import jax
import jax.numpy as jnp
from jax import lax
from jax.experimental import pallas as pl
from jax.experimental.pallas import tpu as pltpu
from jax.sharding import PartitionSpec as P

MESH = pl.DeviceIdType.MESH
F32, BF16 = jnp.float32, jnp.bfloat16
diag_shift = 0.01
EXTRA = 128
PAD = 16


def total(x):
    return jnp.sum(jnp.sum(x, axis=0, keepdims=True), axis=1, keepdims=True)


def kernel(
    groups, shards,
    packed_ref, weight_ref, bias_ref, force_ref, force_b_ref,
    out_ref, out_b_ref,
    packed, weight_t, bias_t, tile, spins, hidden, force_other, lhs, scaled,
    image, image_other, residual, residual_b, by_group, by_shard,
    packed_send, packed_recv, force_sem, image_send, image_recv,
    group_send, group_recv, shard_send, shard_recv,
):
    grp, smp = lax.axis_index("grp"), lax.axis_index("smp")
    chips = shards // 2
    core, chip = lax.rem(smp, 2), smp // 2
    sibling = smp + 1 - 2 * core
    words, here = packed_ref.shape
    units, rows = weight_ref.shape[1], force_ref.shape[0]
    pair = 2 * rows
    samples = chips * here
    count = samples * 2
    block = hidden_block = min(512, units)
    part = image.shape[2]
    parts = units // part

    barrier = pltpu.get_barrier_semaphore()
    for step in range(1, groups):
        pl.semaphore_signal(barrier, device_id={"grp": lax.rem(grp + step, groups)}, device_id_type=MESH)
    for step in range(1, shards):
        pl.semaphore_signal(barrier, device_id={"smp": lax.rem(smp + step, shards)}, device_id_type=MESH)
    pl.semaphore_wait(barrier, groups + shards - 2)

    packed_copies = []
    for step in range(1, chips):
        peer = lax.rem(chip + step, chips)
        packed_copies.append(
            pltpu.make_async_remote_copy(
                packed_ref, packed.at[chip], packed_send.at[step], packed_recv.at[chip],
                device_id={"smp": 2 * peer + core}, device_id_type=MESH,
            )
        )
        packed_copies[-1].start()
    force_copy = pltpu.make_async_remote_copy(
        force_ref, force_other, force_sem.at[0], force_sem.at[1],
        device_id={"smp": sibling}, device_id_type=MESH,
    )
    force_copy.start()
    packed[chip] = packed_ref[...]

    def turn(at, carry):
        cols = pl.ds(pl.multiple_of(at * 256, 256), 256)
        weight_t[cols, :] = weight_ref[:, cols].T
        bias_t[cols, :] = jnp.broadcast_to(bias_ref[:, cols], (128, 256)).T
        return carry

    lax.fori_loop(0, units // 256, turn, 0)

    def own_rows(of):
        return pl.ds(pl.multiple_of(of * rows, rows), rows)

    zero_rows = jnp.zeros((PAD - 1, units), F32)
    lhs[pl.ds(pair, PAD), :] = jnp.concatenate([force_b_ref[...] / chips, zero_rows], axis=0).astype(BF16)
    lhs[own_rows(core), :] = force_ref[...].astype(BF16)
    force_copy.wait()
    lhs[own_rows(1 - core), :] = force_other[...].astype(BF16)

    shifts = lax.broadcasted_iota(jnp.int32, (32, block), 0)
    tiles = here // block

    def values_of(cols):
        projected = jnp.dot(lhs[...], hidden[:, cols], preferred_element_type=F32)
        value = jnp.sum(projected[:pair] * spins[:, cols].astype(F32), axis=0, keepdims=True)
        return value + projected[pair : pair + 1]

    def hidden_block_of(at_chip, turn_at, carry):
        local = pl.ds(pl.multiple_of(turn_at * block, block), block)
        cols = pl.ds(pl.multiple_of(at_chip * here + turn_at * block, block), block)
        for word in range(words):
            bits = jnp.right_shift(jnp.broadcast_to(packed[at_chip, word : word + 1, local], (32, block)), shifts)
            tile[word * 32 : word * 32 + 32, :] = (2 * jnp.bitwise_and(bits, 1) - 1).astype(F32).astype(BF16)
        spins[:, cols] = tile[pl.ds(pl.multiple_of(chip * pair, pair), pair), :]
        for unit in range(0, units, hidden_block):
            these = pl.ds(unit, hidden_block)
            pre = jnp.dot(weight_t[these, :], tile[...], preferred_element_type=F32)
            bias = bias_t[these, :]
            pre = pre + jnp.concatenate([bias] * (block // 128), axis=1)
            hidden[these, cols] = jnp.tanh(pre).astype(BF16)
        by_group[0, grp, :, cols] = values_of(cols)
        return carry

    for step in range(chips):
        at_chip = lax.rem(chip + chips - step, chips)
        if step:
            pltpu.make_async_remote_copy(
                packed_ref, packed.at[at_chip], packed_send.at[step], packed_recv.at[at_chip],
                device_id={"smp": sibling}, device_id_type=MESH,
            ).wait_recv()
        lax.fori_loop(0, tiles, functools.partial(hidden_block_of, at_chip), 0)
    for copy in packed_copies:
        copy.wait_send()

    def gather(slots, which, axis, size, me, send, recv):
        copies = []
        for step in range(1, size):
            copies.append(
                pltpu.make_async_remote_copy(
                    slots.at[which, me], slots.at[which, me], send.at[which, step], recv.at[which, me],
                    device_id={axis: lax.rem(me + step, size)}, device_id_type=MESH,
                )
            )
            copies[-1].start()
        for step in range(1, size):
            source = lax.rem(me + size - step, size)
            pltpu.make_async_remote_copy(
                slots.at[which, source], slots.at[which, source], send.at[which, step], recv.at[which, source],
                device_id={axis: source}, device_id_type=MESH,
            ).wait_recv()
        for copy in copies:
            copy.wait_send()

    lane = lax.broadcasted_iota(jnp.int32, (1, EXTRA), 1)

    def reduce_values(which, first, second):
        by_group[which, grp, :, samples:] = jnp.where(lane == 0, first, jnp.where(lane == 1, second, 0.0))
        gather(by_group, which, "grp", groups, grp, group_send, group_recv)
        mine = by_group[which, 0]
        for source in range(1, groups):
            mine = mine + by_group[which, source]
        by_shard[which, smp] = mine
        gather(by_shard, which, "smp", shards, smp, shard_send, shard_recv)
        halves = []
        for half in range(2):
            value = by_shard[which, half]
            for source in range(half + 2, shards, 2):
                value = value + by_shard[which, source]
            halves.append(value)
        extra = halves[0][:, samples:] + halves[1][:, samples:]
        first = jnp.sum(jnp.where(lane == 0, extra, 0.0), axis=1, keepdims=True)
        second = jnp.sum(jnp.where(lane == 1, extra, 0.0), axis=1, keepdims=True)
        return halves[0][:, :samples], halves[1][:, :samples], first, second

    def centre(low, high):
        mean = total(low) / count + total(high) / count
        return low - mean, high - mean

    force_dot = total(force_ref[...] * force_ref[...]) + total(force_b_ref[...] * force_b_ref[...]) / shards
    low0, high0, norm0, _ = reduce_values(0, force_dot, jnp.zeros((1, 1), F32))
    low, high = centre(low0, high0)
    curvature0 = total(low * low) / count + total(high * high) / count + diag_shift * norm0
    step0 = norm0 / curvature0

    mine = (jnp.where(core == 0, low, high)).astype(F32)
    for at in range(0, samples, block):
        weights = mine[:, at : at + block]
        scaled[:pair, at : at + block] = (spins[:, at : at + block].astype(F32) * weights).astype(BF16)
        scaled[pair:, at : at + block] = jnp.concatenate(
            [weights, jnp.zeros((PAD - 1, block), F32)], axis=0
        ).astype(BF16)

    def image_copy(at):
        return pltpu.make_async_remote_copy(
            image.at[at], image_other.at[at], image_send.at[at], image_recv.at[at],
            device_id={"smp": sibling}, device_id_type=MESH,
        )

    def image_part(at, carry):
        these = pl.ds(pl.multiple_of(at * part, part), part)
        image[at] = lax.dot_general(
            scaled[...], hidden[these, :], (((1,), (1,)), ((), ())), preferred_element_type=F32
        )
        image_copy(at).start()
        return carry

    lax.fori_loop(0, parts, image_part, 0)

    scale = 1.0 / count

    def residual_part(at, carry):
        first, second = carry
        these = pl.ds(pl.multiple_of(at * part, part), part)
        image_copy(at).wait()

        def next_residual(which, force):
            whole = image[at, which, :] + image_other[at, which, :]
            return force - step0 * (whole * scale + diag_shift * force)

        own = next_residual(own_rows(core), force_ref[:, these])
        residual[:, these] = own
        lhs[own_rows(core), these] = own.astype(BF16)
        lhs[own_rows(1 - core), these] = next_residual(own_rows(1 - core), force_other[:, these]).astype(BF16)
        own_b = next_residual(pl.ds(pair, 1), force_b_ref[:, these])
        residual_b[:, these] = own_b
        lhs[pl.ds(pair, PAD), these] = jnp.concatenate([own_b / chips, jnp.zeros((PAD - 1, part), F32)], axis=0).astype(BF16)
        first = first + total(own * own) + total(own_b * own_b) / shards
        second = second + total(own * force_ref[:, these]) + total(own_b * force_b_ref[:, these]) / shards
        return first, second

    zero = jnp.zeros((1, 1), F32)
    own_norm, own_cross = lax.fori_loop(0, parts, residual_part, (zero, zero))

    def second_values(at, carry):
        cols = pl.ds(pl.multiple_of(at * block, block), block)
        by_group[1, grp, :, cols] = values_of(cols)
        return carry

    lax.fori_loop(0, samples // block, second_values, 0)
    low1, high1, norm1, cross = reduce_values(1, own_norm, own_cross)
    beta = norm1 / norm0
    low, high = centre(low1 + beta * low0, high1 + beta * high0)
    direction_dot = norm1 + 2.0 * beta * cross + beta * beta * norm0
    curvature1 = total(low * low) / count + total(high * high) / count + diag_shift * direction_dot
    step1 = norm1 / curvature1

    out_ref[...] = step0 * force_ref[...] + step1 * (residual[...] + beta * force_ref[...])
    out_b_ref[...] = step0 * force_b_ref[...] + step1 * (residual_b[...] + beta * force_b_ref[...])


def body(groups, shards, spins_packed, weight, hidden_bias, force_w, force_b):
    words, here = spins_packed.shape
    inputs, units = weight.shape
    rows = force_w.shape[0]
    chips = shards // 2
    samples, pair = chips * here, 2 * rows
    part = 256
    parts = units // part
    vmem = pl.BlockSpec(memory_space=pltpu.VMEM)
    dma = pltpu.SemaphoreType.DMA
    update_w, update_b = pl.pallas_call(
        functools.partial(kernel, groups, shards),
        out_shape=(jax.ShapeDtypeStruct((rows, units), F32), jax.ShapeDtypeStruct((1, units), F32)),
        in_specs=[vmem] * 5,
        out_specs=(vmem, vmem),
        scratch_shapes=[
            pltpu.VMEM((chips, words, here), jnp.int32),
            pltpu.VMEM((units, inputs), BF16),
            pltpu.VMEM((units, 128), F32),
            pltpu.VMEM((inputs, min(512, units)), BF16),
            pltpu.VMEM((pair, samples), BF16),
            pltpu.VMEM((units, samples), BF16),
            pltpu.VMEM((rows, units), F32),
            pltpu.VMEM((pair + PAD, units), BF16),
            pltpu.VMEM((pair + PAD, samples), BF16),
            pltpu.VMEM((parts, pair + PAD, part), F32),
            pltpu.VMEM((parts, pair + PAD, part), F32),
            pltpu.VMEM((rows, units), F32),
            pltpu.VMEM((1, units), F32),
            pltpu.VMEM((2, groups, 1, samples + EXTRA), F32),
            pltpu.VMEM((2, shards, 1, samples + EXTRA), F32),
            dma((chips,)),
            dma((chips,)),
            dma((2,)),
            dma((parts,)),
            dma((parts,)),
            dma((2, groups)),
            dma((2, groups)),
            dma((2, shards)),
            dma((2, shards)),
        ],
        compiler_params=pltpu.CompilerParams(
            collective_id=0, has_side_effects=True, vmem_limit_bytes=62 * 1024 * 1024
        ),
    )(spins_packed, weight, hidden_bias.reshape(1, -1), force_w, force_b.reshape(1, -1))
    return update_w, update_b.reshape(-1)


def solution(mesh):
    placed = (P(None, "smp"), P(None, "grp"), P("grp"), P("smp", "grp"), P("grp"))
    return jax.shard_map(
        functools.partial(body, mesh.shape["grp"], mesh.shape["smp"]),
        mesh=mesh, in_specs=placed, out_specs=(P("smp", "grp"), P("grp")), check_vma=False,
    )
```

profile of v0, /device:TPU:0, one launch (start us, length us, event | category | flops | bytes accessed | tf_op | source)
XLA Modules:
  0.0 70.7 jit_solution(540424459916573371)
XLA Ops:
  0.6 66.4 %shard_map.68 = (f32[128,2048]{1,0:T(8,128)}, f32[1,2048]{1,0:T(1,128)}) custom-call(s32[32,1024]{1,0:T(8,128)} %packed_ref.1, bf16[1024,2048]{1,0:T(8,128)(2,1)} %weight_ref.1, f32[1,2048]{1,0:T(1,128)} %bitcast.3, f32[128,2048]{1,0:T(8,128)} %force_ref.1, f32[1,2048]{1,0:T(1,128)} %bitcast.4), custom_call_target="tpu_custom_call" | custom-call | tf_op jit(solution)/shard_map/pallas_call | solution.py:245
  67.1 2.3 %copy.9 = f32[128,2048]{1,0:T(8,128)} copy(f32[128,2048]{1,0:T(8,128)} %get-tuple-element.8) | data formatting | bytes 2097152
  69.4 1.3 %copy.10 = f32[2048]{0:T(1024)} copy(f32[2048]{0:T(1024)} %bitcast.5) | data formatting | bytes 16384
where the time goes:
time: 70.9 us; the launch traced here: 70.7 us
  Pallas kernels  66.4 us (94%)
  local copies, waits for them, and re-layouts  3.59 us (5%)
    pallas_call x1, Pallas kernels, body(): pl.pallas_call(functools.partial(kernel, groups, shards), out_shape=(jax....  66.4 us
    unnamed x2, local copies, waits for them, and re-layouts  3.59 us

commit v1 on v0

v1 whole, which is shorter than its diff:
```python
import functools

import jax
import jax.numpy as jnp
from jax import lax
from jax.experimental import pallas as pl
from jax.experimental.pallas import tpu as pltpu
from jax.sharding import PartitionSpec as P

MESH = pl.DeviceIdType.MESH
F32, BF16 = jnp.float32, jnp.bfloat16
diag_shift = 0.01
EXTRA = 128
PAD = 16
CHUNKS = 4


def total(x):
    return jnp.sum(jnp.sum(x, axis=0, keepdims=True), axis=1, keepdims=True)


def kernel(
    groups, shards,
    packed_hbm, weight_hbm, bias_ref, force_hbm, force_b_ref,
    out_ref, out_b_ref,
    packed, weight_in, weight_t, bias_t, tile, spins, hidden, force_own, force_pair, lhs, scaled,
    image, image_other, res_own, res_send, res_recv, by_group, by_shard,
    load_sem, spread_send, spread_recv, share_send, share_recv,
    sib_sem, cross_send, cross_recv, relay_send, relay_recv,
    image_send, image_recv, res_send_sem, res_recv_sem,
    group_send, group_recv, shard_send, shard_recv,
):
    grp, smp = lax.axis_index("grp"), lax.axis_index("smp")
    chips = shards // 2
    pairs = chips // 2
    core, chip = lax.rem(smp, 2), smp // 2
    pair_at, side = chip // 2, lax.rem(chip, 2)
    sibling = smp + 1 - 2 * core
    partner = smp + 2 - 4 * side
    words, here = packed_hbm.shape
    rows, units = force_hbm.shape
    half = units // 2
    both = 2 * rows
    wide = 4 * rows
    samples = chips * here
    count = samples * 2
    block = min(512, here)
    part = image.shape[2]
    parts = half // part
    slice_ = here // groups
    chunk = half // CHUNKS
    tiles = here // block
    turns = chips * tiles

    loads = [
        pltpu.make_async_copy(packed_hbm, packed.at[chip], load_sem.at[0]),
        pltpu.make_async_copy(force_hbm, force_own, load_sem.at[1]),
        pltpu.make_async_copy(
            weight_hbm.at[:, pl.ds(pl.multiple_of(side * half, half), half)], weight_in, load_sem.at[2]
        ),
    ]
    for load in loads:
        load.start()

    barrier = pltpu.get_barrier_semaphore()
    for step in range(1, groups):
        pl.semaphore_signal(barrier, device_id={"grp": lax.rem(grp + step, groups)}, device_id_type=MESH)
    for step in range(1, shards):
        pl.semaphore_signal(barrier, device_id={"smp": lax.rem(smp + step, shards)}, device_id_type=MESH)

    def chip_of(step):
        return lax.rem(pair_at + step // 2, pairs) * 2 + lax.rem(side + lax.rem(step, 2), 2)

    def quarter(of):
        return pl.ds(pl.multiple_of(of * slice_, slice_), slice_)

    def spread(step, source, target):
        return pltpu.make_async_remote_copy(
            packed.at[source, :, quarter(grp)], packed.at[source, :, quarter(grp)],
            spread_send.at[step], spread_recv.at[source],
            device_id={"smp": 2 * target + core}, device_id_type=MESH,
        )

    def share(source, step):
        return pltpu.make_async_remote_copy(
            packed.at[source, :, quarter(grp)], packed.at[source, :, quarter(grp)],
            share_send.at[source, step], share_recv.at[source, grp],
            device_id={"grp": lax.rem(grp + step, groups)}, device_id_type=MESH,
        )

    def shared(source, of):
        return pltpu.make_async_remote_copy(
            packed.at[source, :, quarter(of)], packed.at[source, :, quarter(of)],
            share_send.at[source, 0], share_recv.at[source, of],
            device_id={"grp": of}, device_id_type=MESH,
        )

    mine_at = pl.multiple_of(side * half, half)
    theirs_at = pl.multiple_of((1 - side) * half, half)
    mine_cols, their_cols = pl.ds(mine_at, half), pl.ds(theirs_at, half)

    def core_rows(base, of):
        return pl.ds(pl.multiple_of(base + of * rows, rows), rows)

    def sib_copy():
        return pltpu.make_async_remote_copy(
            force_own.at[:, mine_cols], force_pair.at[core_rows(both, core), :], sib_sem.at[0], sib_sem.at[1],
            device_id={"smp": sibling}, device_id_type=MESH,
        )

    def cross(at):
        return pltpu.make_async_remote_copy(
            force_own.at[:, pl.ds(pl.multiple_of(theirs_at + at * chunk, chunk), chunk)],
            force_pair.at[core_rows(0, core), pl.ds(at * chunk, chunk)],
            cross_send.at[at], cross_recv.at[at],
            device_id={"smp": partner}, device_id_type=MESH,
        )

    def relay(at):
        where = force_pair.at[core_rows(0, core), pl.ds(at * chunk, chunk)]
        return pltpu.make_async_remote_copy(
            where, where, relay_send.at[at], relay_recv.at[at],
            device_id={"smp": sibling}, device_id_type=MESH,
        )

    loads[2].wait()
    step_w = min(256, half)

    def turn(at, carry):
        cols = pl.ds(pl.multiple_of(at * step_w, step_w), step_w)
        far = pl.ds(pl.multiple_of(mine_at + at * step_w, step_w), step_w)
        weight_t[cols, :] = weight_in[:, cols].T
        bias_t[cols, :] = jnp.broadcast_to(bias_ref[:, far], (128, step_w)).T
        return carry

    lax.fori_loop(0, half // step_w, turn, 0)
    loads[0].wait()
    loads[1].wait()
    pl.semaphore_wait(barrier, groups + shards - 2)
    for step in range(1, chips):
        spread(step, chip, chip_of(step)).start()
    sib_copy().start()
    for at in range(CHUNKS):
        cross(at).start()

    zero_rows = jnp.zeros((PAD - 1, half), F32)
    lhs[pl.ds(wide, PAD), :] = jnp.concatenate([force_b_ref[:, mine_cols] / pairs, zero_rows], axis=0).astype(BF16)
    mine_force = force_own[:, mine_cols]
    force_pair[core_rows(both, core), :] = mine_force
    lhs[core_rows(both, core), :] = mine_force.astype(BF16)
    sib_copy().wait()
    lhs[core_rows(both, 1 - core), :] = force_pair[core_rows(both, 1 - core), :].astype(BF16)

    shifts = lax.broadcasted_iota(jnp.int32, (32, block), 0)

    def own_values(cols):
        projected = jnp.dot(lhs[both:, :], hidden[:, cols], preferred_element_type=F32)
        value = jnp.sum(projected[:both] * spins[both:, cols].astype(F32), axis=0, keepdims=True)
        return value + projected[both : both + 1]

    def far_values(cols):
        projected = jnp.dot(lhs[:both, :], hidden[:, cols], preferred_element_type=F32)
        return jnp.sum(projected * spins[:both, cols].astype(F32), axis=0, keepdims=True)

    def values_of(cols):
        projected = jnp.dot(lhs[...], hidden[:, cols], preferred_element_type=F32)
        value = jnp.sum(projected[:wide] * spins[:, cols].astype(F32), axis=0, keepdims=True)
        return value + projected[wide : wide + 1]

    unit_block = min(512, half)

    def hidden_block(turn_at, carry):
        step = turn_at // tiles
        at_chip = chip_of(step)
        in_chip = lax.rem(turn_at, tiles)

        def forward(step):
            spread(step, chip_of(step), chip).wait_recv()
            for peer in range(1, groups):
                share(chip_of(step), peer).start()

        @pl.when(turn_at == 1)
        def _():
            forward(1)

        @pl.when(turn_at == min(2, turns - 1))
        def _():
            for step in range(2, chips):
                forward(step)

        @pl.when((in_chip == 0) & (step > 0))
        def _():
            for peer in range(1, groups):
                shared(at_chip, lax.rem(grp + groups - peer, groups)).wait_recv()

        for at in range(CHUNKS):

            @pl.when(turn_at == turns - CHUNKS + at)
            def _(at=at):
                cross(at).wait_recv()
                relay(at).start()

        local = pl.ds(pl.multiple_of(in_chip * block, block), block)
        cols = pl.ds(pl.multiple_of(at_chip * here + in_chip * block, block), block)
        for word in range(words):
            bits = jnp.right_shift(jnp.broadcast_to(packed[at_chip, word : word + 1, local], (32, block)), shifts)
            tile[word * 32 : word * 32 + 32, :] = (2 * jnp.bitwise_and(bits, 1) - 1).astype(F32).astype(BF16)
        spins[:both, cols] = tile[pl.ds(pl.multiple_of((chip + 1 - 2 * side) * both, both), both), :]
        spins[both:, cols] = tile[pl.ds(pl.multiple_of(chip * both, both), both), :]
        for unit in range(0, half, unit_block):
            these = pl.ds(unit, unit_block)
            pre = jnp.dot(weight_t[these, :], tile[...], preferred_element_type=F32)
            bias = bias_t[these, :]
            pre = pre + jnp.concatenate([bias] * (block // 128), axis=1)
            hidden[these, cols] = jnp.tanh(pre).astype(BF16)
        by_group[0, grp, :, cols] = own_values(cols)
        return carry

    lax.fori_loop(0, turns, hidden_block, 0)

    for at in range(CHUNKS):
        relay(at).wait_recv()
    lhs[:both, :] = force_pair[:both, :].astype(BF16)

    def rest_of_values(at, carry):
        cols = pl.ds(pl.multiple_of(at * block, block), block)
        by_group[0, grp, :, cols] = by_group[0, grp, :, cols] + far_values(cols)
        return carry

    lax.fori_loop(0, samples // block, rest_of_values, 0)

    for step in range(1, chips):
        spread(step, chip, chip_of(step)).wait_send()
        for peer in range(1, groups):
            share(chip_of(step), peer).wait_send()
    for at in range(CHUNKS):
        cross(at).wait_send()
        relay(at).wait_send()

    def gather(slots, which, axis, size, me, send, recv):
        copies = []
        for step in range(1, size):
            copies.append(
                pltpu.make_async_remote_copy(
                    slots.at[which, me], slots.at[which, me], send.at[which, step], recv.at[which, me],
                    device_id={axis: lax.rem(me + step, size)}, device_id_type=MESH,
                )
            )
            copies[-1].start()
        for step in range(1, size):
            source = lax.rem(me + size - step, size)
            pltpu.make_async_remote_copy(
                slots.at[which, source], slots.at[which, source], send.at[which, step], recv.at[which, source],
                device_id={axis: source}, device_id_type=MESH,
            ).wait_recv()
        for copy in copies:
            copy.wait_send()

    lane = lax.broadcasted_iota(jnp.int32, (1, EXTRA), 1)

    def reduce_values(which, first, second):
        by_group[which, grp, :, samples:] = jnp.where(lane == 0, first, jnp.where(lane == 1, second, 0.0))
        gather(by_group, which, "grp", groups, grp, group_send, group_recv)
        mine = by_group[which, 0]
        for source in range(1, groups):
            mine = mine + by_group[which, source]
        by_shard[which, smp] = mine
        gather(by_shard, which, "smp", shards, smp, shard_send, shard_recv)
        halves = []
        for parity in range(2):
            value = by_shard[which, parity]
            for source in range(parity + 2, shards, 2):
                value = value + by_shard[which, source]
            halves.append(value)
        extra = halves[0][:, samples:] + halves[1][:, samples:]
        first = jnp.sum(jnp.where(lane == 0, extra, 0.0), axis=1, keepdims=True)
        second = jnp.sum(jnp.where(lane == 1, extra, 0.0), axis=1, keepdims=True)
        return halves[0][:, :samples], halves[1][:, :samples], first, second

    def centre(low, high):
        mean = total(low) / count + total(high) / count
        return low - mean, high - mean

    force_dot = total(force_own[...] * force_own[...]) + total(force_b_ref[...] * force_b_ref[...]) / shards
    low0, high0, norm0, _ = reduce_values(0, force_dot, jnp.zeros((1, 1), F32))
    low, high = centre(low0, high0)
    curvature0 = total(low * low) / count + total(high * high) / count + diag_shift * norm0
    step0 = norm0 / curvature0

    mine = jnp.where(core == 0, low, high)
    for at in range(0, samples, block):
        weights = mine[:, at : at + block]
        scaled[:wide, at : at + block] = (spins[:, at : at + block].astype(F32) * weights).astype(BF16)
        scaled[wide:, at : at + block] = jnp.concatenate(
            [weights, jnp.zeros((PAD - 1, block), F32)], axis=0
        ).astype(BF16)

    def image_copy(at):
        return pltpu.make_async_remote_copy(
            image.at[at], image_other.at[at], image_send.at[at], image_recv.at[at],
            device_id={"smp": sibling}, device_id_type=MESH,
        )

    def image_part(at, carry):
        these = pl.ds(pl.multiple_of(at * part, part), part)
        image[at] = lax.dot_general(
            scaled[...], hidden[these, :], (((1,), (1,)), ((), ())), preferred_element_type=F32
        )
        image_copy(at).start()
        return carry

    lax.fori_loop(0, parts, image_part, 0)

    scale = 1.0 / count
    held = shards // 2

    def res_copy(at):
        return pltpu.make_async_remote_copy(
            res_send.at[at], res_recv.at[at], res_send_sem.at[at], res_recv_sem.at[at],
            device_id={"smp": partner}, device_id_type=MESH,
        )

    def residual_part(at, carry):
        first, second = carry
        these = pl.ds(pl.multiple_of(at * part, part), part)
        image_copy(at).wait()

        def next_residual(which, force):
            whole = image[at, which, :] + image_other[at, which, :]
            return force - step0 * (whole * scale + diag_shift * force)

        force_far, force_near = force_pair[core_rows(0, core), these], force_pair[core_rows(both, core), these]
        far, near = next_residual(core_rows(0, core), force_far), next_residual(core_rows(both, core), force_near)
        force_b = force_b_ref[:, pl.ds(pl.multiple_of(mine_at + at * part, part), part)]
        own_b = next_residual(pl.ds(wide, 1), force_b)
        res_send[at, :rows, :] = far
        res_send[at, rows:, :] = jnp.broadcast_to(own_b, (8, part))
        res_copy(at).start()
        res_own[at, :rows, :] = near
        res_own[at, rows:, :] = jnp.broadcast_to(own_b, (8, part))
        lhs[core_rows(0, core), these] = far.astype(BF16)
        lhs[core_rows(both, core), these] = near.astype(BF16)
        for base in (0, both):
            which = core_rows(base, 1 - core)
            lhs[which, these] = next_residual(which, force_pair[which, these]).astype(BF16)
        lhs[pl.ds(wide, PAD), these] = jnp.concatenate([own_b / pairs, jnp.zeros((PAD - 1, part), F32)], axis=0).astype(BF16)
        first = first + total(far * far) + total(near * near) + total(own_b * own_b) / held
        second = second + total(far * force_far) + total(near * force_near) + total(own_b * force_b) / held
        return first, second

    zero = jnp.zeros((1, 1), F32)
    own_norm, own_cross = lax.fori_loop(0, parts, residual_part, (zero, zero))

    def second_values(at, carry):
        cols = pl.ds(pl.multiple_of(at * block, block), block)
        by_group[1, grp, :, cols] = values_of(cols)
        return carry

    lax.fori_loop(0, samples // block, second_values, 0)
    low1, high1, norm1, crossed = reduce_values(1, own_norm, own_cross)
    beta = norm1 / norm0
    low, high = centre(low1 + beta * low0, high1 + beta * high0)
    direction_dot = norm1 + 2.0 * beta * crossed + beta * beta * norm0
    curvature1 = total(low * low) / count + total(high * high) / count + diag_shift * direction_dot
    step1 = norm1 / curvature1

    of_force = step0 + step1 * beta
    for at in range(parts):
        res_copy(at).wait()
        for base, held_in in ((mine_at, res_own), (theirs_at, res_recv)):
            cols = pl.ds(pl.multiple_of(base + at * part, part), part)
            out_ref[:, cols] = of_force * force_own[:, cols] + step1 * held_in[at, :rows, :]
            out_b_ref[:, cols] = of_force * force_b_ref[:, cols] + step1 * held_in[at, rows : rows + 1, :]


def body(groups, shards, spins_packed, weight, hidden_bias, force_w, force_b):
    words, here = spins_packed.shape
    inputs, units = weight.shape
    rows = force_w.shape[0]
    chips = shards // 2
    samples, wide, half = chips * here, 4 * rows, units // 2
    part = min(256, half)
    parts = half // part
    vmem = pl.BlockSpec(memory_space=pltpu.VMEM)
    hbm = pl.BlockSpec(memory_space=pl.ANY)
    dma = pltpu.SemaphoreType.DMA
    update_w, update_b = pl.pallas_call(
        functools.partial(kernel, groups, shards),
        out_shape=(jax.ShapeDtypeStruct((rows, units), F32), jax.ShapeDtypeStruct((1, units), F32)),
        in_specs=[hbm, hbm, vmem, hbm, vmem],
        out_specs=(vmem, vmem),
        scratch_shapes=[
            pltpu.VMEM((chips, words, here), jnp.int32),
            pltpu.VMEM((inputs, half), BF16),
            pltpu.VMEM((half, inputs), BF16),
            pltpu.VMEM((half, 128), F32),
            pltpu.VMEM((inputs, min(512, here)), BF16),
            pltpu.VMEM((wide, samples), BF16),
            pltpu.VMEM((half, samples), BF16),
            pltpu.VMEM((rows, units), F32),
            pltpu.VMEM((wide, half), F32),
            pltpu.VMEM((wide + PAD, half), BF16),
            pltpu.VMEM((wide + PAD, samples), BF16),
            pltpu.VMEM((parts, wide + PAD, part), F32),
            pltpu.VMEM((parts, wide + PAD, part), F32),
            pltpu.VMEM((parts, rows + 8, part), F32),
            pltpu.VMEM((parts, rows + 8, part), F32),
            pltpu.VMEM((parts, rows + 8, part), F32),
            pltpu.VMEM((2, groups, 1, samples + EXTRA), F32),
            pltpu.VMEM((2, shards, 1, samples + EXTRA), F32),
            dma((3,)),
            dma((chips,)),
            dma((chips,)),
            dma((chips, groups)),
            dma((chips, groups)),
            dma((2,)),
            dma((CHUNKS,)),
            dma((CHUNKS,)),
            dma((CHUNKS,)),
            dma((CHUNKS,)),
            dma((parts,)),
            dma((parts,)),
            dma((parts,)),
            dma((parts,)),
            dma((2, groups)),
            dma((2, groups)),
            dma((2, shards)),
            dma((2, shards)),
        ],
        compiler_params=pltpu.CompilerParams(
            collective_id=0, has_side_effects=True, vmem_limit_bytes=62 * 1024 * 1024
        ),
    )(spins_packed, weight, hidden_bias.reshape(1, -1), force_w, force_b.reshape(1, -1))
    return update_w, update_b.reshape(-1)


def solution(mesh):
    placed = (P(None, "smp"), P(None, "grp"), P("grp"), P("smp", "grp"), P("grp"))
    return jax.shard_map(
        functools.partial(body, mesh.shape["grp"], mesh.shape["smp"]),
        mesh=mesh, in_specs=placed, out_specs=(P("smp", "grp"), P("grp")), check_vma=False,
    )
```

time: 70.9 us -> 65.8 us (0.928)
  Pallas kernels: 66.4 us -> 61.3 us
    pallas_call x1, Pallas kernels: 66.4 us -> 61.3 us  [body(): pl.pallas_call(functools.partial(kernel, groups, shards), out_shape=(jax....]
where the time goes in v1:
time: 65.8 us; the launch traced here: 65.5 us
  Pallas kernels  61.3 us (93%)
  local copies, waits for them, and re-layouts  3.59 us (5%)
    pallas_call x1, Pallas kernels, body(): pl.pallas_call(functools.partial(kernel, groups, shards), out_shape=(jax....  61.3 us
    unnamed x2, local copies, waits for them, and re-layouts  3.59 us

profile of v1, /device:TPU:0, one launch (start us, length us, event | category | flops | bytes accessed | tf_op | source)
XLA Modules:
  0.0 65.5 jit_solution(14931532767357189294)
XLA Ops:
  0.6 61.3 %shard_map.68 = (f32[128,2048]{1,0:T(8,128)}, f32[1,2048]{1,0:T(1,128)}) custom-call(s32[32,1024]{1,0:T(8,128)} %packed_hbm.1, bf16[1024,2048]{1,0:T(8,128)(2,1)} %weight_hbm.1, f32[1,2048]{1,0:T(1,128)} %bitcast.3, f32[128,2048]{1,0:T(8,128)} %force_hbm.1, f32[1,2048]{1,0:T(1,128)} %bitcast.4), custom_call_target="tpu_custom_call" | custom-call | tf_op jit(solution)/shard_map/pallas_call | solution.py:387
  61.9 2.3 %copy.9 = f32[128,2048]{1,0:T(8,128)} copy(f32[128,2048]{1,0:T(8,128)} %get-tuple-element.8) | data formatting | bytes 2097152
  64.2 1.3 %copy.10 = f32[2048]{0:T(1024)} copy(f32[2048]{0:T(1024)} %bitcast.5) | data formatting | bytes 16384

commit v2 on v0

v2 whole, which is shorter than its diff:
```python
import functools

import jax
import jax.numpy as jnp
from jax import lax
from jax.experimental import pallas as pl
from jax.experimental.pallas import tpu as pltpu
from jax.sharding import PartitionSpec as P

MESH = pl.DeviceIdType.MESH
F32, BF16 = jnp.float32, jnp.bfloat16
diag_shift = 0.01
LANES = 128
PAD = 16
BLOCK = 512
UNITS = 512
PART = 256
LAG = 2
FEW = 32


def total(x):
    return jnp.sum(jnp.sum(x, axis=0, keepdims=True), axis=1, keepdims=True)


def each(low, high, step):
    if high - low <= FEW:
        for at in range(low, high):
            step(at)
    else:
        lax.fori_loop(low, high, lambda at, carry: (step(at), carry)[1], 0)


def kernel(
    groups, shards, pieces,
    packed_hbm, weight_hbm, bias_ref, force_hbm, force_b_ref,
    res_hbm, res_b_ref, coef_ref,
    packed, weight_in, weight_t, bias_t, tile, spins, hidden, force_own, force_other, lhs, scaled,
    image, image_other, residual, values, extras, squares,
    load_sem, packed_send, packed_recv, force_sem, image_send, image_recv, store_sem,
    value_send, value_recv, extra_send, extra_recv, square_sem, ready,
):
    grp, smp = lax.axis_index("grp"), lax.axis_index("smp")
    chips = shards // 2
    pairs = chips // 2
    core, chip = lax.rem(smp, 2), smp // 2
    pair_at, side = chip // 2, lax.rem(chip, 2)
    sibling = smp + 1 - 2 * core
    words, here = packed_hbm.shape
    rows, units = force_hbm.shape
    pair = 2 * rows
    samples = chips * here
    count = samples * 2
    block = tile.shape[1]
    unit_block = min(UNITS, units)
    part = image.shape[2]
    parts = units // part
    tiles = here // block
    turns = chips * tiles
    piece = samples // pieces
    peers = groups * chips
    everyone = groups * shards

    loads = [
        pltpu.make_async_copy(packed_hbm, packed.at[chip], load_sem.at[0]),
        pltpu.make_async_copy(force_hbm, force_own, load_sem.at[1]),
    ]
    loads[0].start()
    weight_loads = []
    for unit in range(0, units, unit_block):
        these = pl.ds(unit, unit_block)
        weight_loads.append(
            pltpu.make_async_copy(weight_hbm.at[:, these], weight_in.at[:, these], load_sem.at[2 + unit // unit_block])
        )
        weight_loads[-1].start()
    loads[1].start()

    barrier = pltpu.get_barrier_semaphore()
    for step in range(1, groups):
        pl.semaphore_signal(barrier, device_id={"grp": lax.rem(grp + step, groups)}, device_id_type=MESH)
    for step in range(1, shards):
        pl.semaphore_signal(barrier, device_id={"smp": lax.rem(smp + step, shards)}, device_id_type=MESH)

    def chip_of(step):
        return lax.rem(pair_at + step // 2, pairs) * 2 + lax.rem(side + lax.rem(step, 2), 2)

    def packed_copy(source, target, at):
        where = packed.at[source, :, pl.ds(pl.multiple_of(at * block, block), block)]
        return pltpu.make_async_remote_copy(
            where, where, packed_send, packed_recv.at[source, at],
            device_id={"smp": 2 * target + core}, device_id_type=MESH,
        )

    force_copy = pltpu.make_async_remote_copy(
        force_own, force_other, force_sem.at[0], force_sem.at[1],
        device_id={"smp": sibling}, device_id_type=MESH,
    )

    def own_rows(of):
        return pl.ds(pl.multiple_of(of * rows, rows), rows)

    shifts = 31 - lax.broadcasted_iota(jnp.int32, (32, block), 0)

    def unpack(at_chip, in_chip, cols):
        local = pl.ds(pl.multiple_of(in_chip * block, block), block)
        for word in range(words):
            bits = lax.shift_left(jnp.broadcast_to(packed[at_chip, word : word + 1, local], (32, block)), shifts)
            tile[word * 32 : word * 32 + 32, :] = jnp.where(bits < 0, 1.0, -1.0).astype(BF16)
        spins[:, cols] = tile[pl.ds(pl.multiple_of(chip * pair, pair), pair), :]

    def activate(unit, cols):
        these = pl.ds(unit, unit_block)
        pre = jnp.dot(weight_t[these, :], tile[...], preferred_element_type=F32)
        bias = bias_t[these, :]
        pre = pre + jnp.concatenate([bias] * (block // LANES), axis=1)
        hidden[these, cols] = jnp.tanh(pre).astype(BF16)

    def columns(at_chip, in_chip):
        return pl.ds(pl.multiple_of(at_chip * here + in_chip * block, block), block)

    def values_of(cols):
        projected = jnp.dot(lhs[...], hidden[:, cols], preferred_element_type=F32)
        value = jnp.sum(projected[:pair] * spins[:, cols].astype(F32), axis=0, keepdims=True)
        return value + projected[pair : pair + 1]

    slot = grp * chips + chip

    def peer_of(step):
        return lax.rem(grp + step // chips, groups), lax.rem(chip + lax.rem(step, chips), chips)

    def value_copy(which, at, source, target):
        where = values.at[which, source, :, pl.ds(pl.multiple_of(at * piece, piece), piece)]
        return pltpu.make_async_remote_copy(
            where, where, value_send.at[which], value_recv.at[which],
            device_id={"grp": target[0], "smp": 2 * target[1] + core}, device_id_type=MESH,
        )

    def send_piece(which, at):
        each(1, peers, lambda step: value_copy(which, at, slot, peer_of(step)).start())

    def all_values(which):
        where = values.at[which, pl.ds(0, peers - 1)]
        return pltpu.make_async_remote_copy(
            where, where, value_send.at[which], value_recv.at[which],
            device_id={"smp": sibling}, device_id_type=MESH,
        )

    def extra_copy(which, source, target):
        return pltpu.make_async_remote_copy(
            extras.at[which, source], extras.at[which, source],
            extra_send.at[which], extra_recv.at[which],
            device_id={"grp": target[0], "smp": target[1]}, device_id_type=MESH,
        )

    def all_extras(which):
        where = extras.at[which, pl.ds(0, everyone - 1)]
        return pltpu.make_async_remote_copy(
            where, where, extra_send.at[which], extra_recv.at[which],
            device_id={"smp": sibling}, device_id_type=MESH,
        )

    def all_packed():
        where = packed.at[pl.ds(0, chips - 1)]
        return pltpu.make_async_remote_copy(
            where, where, packed_send, packed_recv.at[chip, 0],
            device_id={"smp": sibling}, device_id_type=MESH,
        )

    def anyone(step):
        return lax.rem(grp + step // shards, groups), lax.rem(smp + lax.rem(step, shards), shards)

    width = min(256, unit_block)
    loads[0].wait()
    unpack(chip, 0, columns(chip, 0))
    for unit in range(0, units, unit_block):
        weight_loads[unit // unit_block].wait()
        for start in range(unit, unit + unit_block, width):
            weight_t[start : start + width, :] = weight_in[:, start : start + width].T
            bias_t[start : start + width, :] = jnp.broadcast_to(bias_ref[:, start : start + width], (LANES, width)).T
        activate(unit, columns(chip, 0))
    loads[1].wait()
    pl.semaphore_wait(barrier, groups + shards - 2)
    for step in range(1, chips):
        for at in range(tiles):
            packed_copy(chip, chip_of(step), at).start()
    force_copy.start()
    for step in range(1, shards):
        pl.semaphore_signal(ready, device_id={"smp": lax.rem(smp + step, shards)}, device_id_type=MESH)
    for at in range(1, tiles):
        unpack(chip, at, columns(chip, at))
        for unit in range(0, units, unit_block):
            activate(unit, columns(chip, at))

    zero_rows = jnp.zeros((PAD - 1, units), F32)
    lhs[pl.ds(pair, PAD), :] = jnp.concatenate([force_b_ref[...] / chips, zero_rows], axis=0).astype(BF16)
    lhs[own_rows(core), :] = force_own[...].astype(BF16)
    force_dot = total(force_own[...] * force_own[...]) + total(force_b_ref[...] * force_b_ref[...]) / shards
    force_copy.wait()
    lhs[own_rows(1 - core), :] = force_other[...].astype(BF16)
    for at in range(tiles):
        values[0, slot, :, columns(chip, at)] = values_of(columns(chip, at))
    pl.semaphore_wait(ready, shards - 1)
    if pieces == turns:
        for at in range(tiles):
            send_piece(0, chip * tiles + at)

    def remote_tile(turn_at, carry):
        at_chip, in_chip = chip_of(turn_at // tiles), lax.rem(turn_at, tiles)
        cols = columns(at_chip, in_chip)
        packed_copy(at_chip, chip, in_chip).wait_recv()
        unpack(at_chip, in_chip, cols)
        for unit in range(0, units, unit_block):
            activate(unit, cols)
        values[0, slot, :, cols] = values_of(cols)
        if pieces == turns:
            send_piece(0, at_chip * tiles + in_chip)
        return carry
    lax.fori_loop(tiles, turns, remote_tile, 0)
    lane = lax.broadcasted_iota(jnp.int32, (1, LANES), 1)

    def reduce_values(which, first, second):
        if pieces < turns:
            for at in range(pieces):
                send_piece(which, at)
        mine = total(values[which, slot])
        extras[which, grp * shards + smp] = jnp.where(
            lane == 0, first, jnp.where(lane == 1, second, jnp.where(lane == 2, mine, 0.0))
        )
        each(1, everyone, lambda step: extra_copy(which, grp * shards + smp, anyone(step)).start())
        all_values(which).wait_recv()
        value = values[which, 0]
        for source in range(1, peers):
            value = value + values[which, source]
        all_extras(which).wait_recv()
        extra = jnp.sum(extras[which], axis=0)

        def pick(at):
            return jnp.sum(jnp.where(lane == at, extra, 0.0), axis=1, keepdims=True)

        return value, pick(0), pick(1), pick(2)

    def drain(which):
        all_values(which).wait_send()
        all_extras(which).wait_send()

    def square_copy(which):
        return pltpu.make_async_remote_copy(
            squares.at[which, 0], squares.at[which, 1], square_sem.at[which, 0], square_sem.at[which, 1],
            device_id={"smp": sibling}, device_id_type=MESH,
        )

    def square_start(which, centred):
        squares[which, 0] = jnp.broadcast_to(total(centred * centred), (8, LANES))
        square_copy(which).start()

    def square_total(which):
        square_copy(which).wait()
        return (squares[which, 0, 0:1, 0:1] + squares[which, 1, 0:1, 0:1]) / count

    value0, norm0, _, sum0 = reduce_values(0, force_dot, jnp.zeros((1, 1), F32))
    centred = value0 - sum0 / count
    square_start(0, centred)

    weights = centred.astype(BF16)
    for at in range(0, samples, block):
        scaled[:pair, at : at + block] = spins[:, at : at + block] * weights[:, at : at + block]
    scaled[pair:, :] = jnp.concatenate([centred, jnp.zeros((PAD - 1, samples), F32)], axis=0).astype(BF16)

    def image_copy(at):
        return pltpu.make_async_remote_copy(
            image.at[at], image_other.at[at], image_send, image_recv.at[at],
            device_id={"smp": sibling}, device_id_type=MESH,
        )

    def image_part(at):
        these = pl.ds(pl.multiple_of(at * part, part), part)
        image[at] = lax.dot_general(
            scaled[...], hidden[these, :], (((1,), (1,)), ((), ())), preferred_element_type=F32
        )
        image_copy(at).start()

    scale = 1.0 / count

    def store(at):
        cols = pl.ds(pl.multiple_of(at * part, part), part)
        return pltpu.make_async_copy(residual.at[:, cols], res_hbm.at[:, cols], store_sem)

    def residual_part(at, step0, norms):
        first, second = norms
        these = pl.ds(pl.multiple_of(at * part, part), part)
        image_copy(at).wait_recv()

        def next_residual(which, force):
            whole = image[at, which, :] + image_other[at, which, :]
            return force - step0 * (whole * scale + diag_shift * force)

        force = force_own[:, these]
        own = next_residual(own_rows(core), force)
        residual[:, these] = own
        lhs[own_rows(core), these] = own.astype(BF16)
        lhs[own_rows(1 - core), these] = next_residual(own_rows(1 - core), force_other[:, these]).astype(BF16)
        force_b = force_b_ref[:, these]
        own_b = next_residual(pl.ds(pair, 1), force_b)
        res_b_ref[:, these] = own_b
        lhs[pl.ds(pair, PAD), these] = jnp.concatenate([own_b / chips, jnp.zeros((PAD - 1, part), F32)], axis=0).astype(BF16)
        store(at).start()
        first = first + jnp.sum(own * own, axis=0, keepdims=True) + own_b * own_b / shards
        second = second + jnp.sum(own * force, axis=0, keepdims=True) + own_b * force_b / shards
        return first, second

    ahead = min(LAG + 1, parts)
    each(0, ahead, image_part)
    step0 = norm0 / (square_total(0) + diag_shift * norm0)
    drain(0)
    all_packed().wait_send()

    def next_part(at, norms):
        norms = residual_part(at - ahead, step0, norms)
        image_part(at)
        return norms

    none = jnp.zeros((1, part), F32)
    norms = lax.fori_loop(ahead, parts, next_part, (none, none))
    norms = lax.fori_loop(parts - ahead, parts, lambda at, norms: residual_part(at, step0, norms), norms)

    def second_values(at, carry):
        cols = pl.ds(pl.multiple_of(at * block, block), block)
        values[1, slot, :, cols] = values_of(cols)
        if pieces == turns:
            send_piece(1, at)
        return carry

    lax.fori_loop(0, turns, second_values, 0)
    own_norm, own_cross = total(norms[0]), total(norms[1])
    value1, norm1, crossed, sum1 = reduce_values(1, own_norm, own_cross)
    beta = norm1 / norm0
    square_start(1, value1 + beta * value0 - (sum1 + beta * sum0) / count)
    drain(1)
    pltpu.make_async_copy(residual, res_hbm, store_sem).wait()
    pltpu.make_async_remote_copy(
        image, image_other, image_send, image_recv.at[0], device_id={"smp": sibling}, device_id_type=MESH
    ).wait_send()
    direction_dot = norm1 + 2.0 * beta * crossed + beta * beta * norm0
    step1 = norm1 / (square_total(1) + diag_shift * direction_dot)
    coef_ref[...] = jnp.where(lane == 0, step0 + step1 * beta, step1)


def finish(force_ref, force_b_ref, res_ref, res_b_ref, coef_ref, out_ref, out_b_ref):
    of_force, step1 = coef_ref[0:1, 0:1], coef_ref[0:1, 1:2]
    out_ref[...] = of_force * force_ref[...] + step1 * res_ref[...]
    out_b_ref[...] = of_force * force_b_ref[...] + step1 * res_b_ref[...]


def body(groups, shards, spins_packed, weight, hidden_bias, force_w, force_b):
    words, here = spins_packed.shape
    inputs, units = weight.shape
    rows = force_w.shape[0]
    chips = shards // 2
    samples, pair = chips * here, 2 * rows
    part = min(PART, units)
    parts = units // part
    block = min(BLOCK, here)
    turns = samples // block
    peers = groups * chips
    pieces = turns if peers <= FEW else 1
    vmem = pl.BlockSpec(memory_space=pltpu.VMEM)
    hbm = pl.BlockSpec(memory_space=pl.ANY)
    dma = pltpu.SemaphoreType.DMA
    bias_row, force_row = hidden_bias.reshape(1, -1), force_b.reshape(1, -1)
    wide, thin = jax.ShapeDtypeStruct((rows, units), F32), jax.ShapeDtypeStruct((1, units), F32)
    res, res_b, coef = pl.pallas_call(
        functools.partial(kernel, groups, shards, pieces),
        out_shape=(wide, thin, jax.ShapeDtypeStruct((1, LANES), F32)),
        in_specs=[hbm, hbm, vmem, hbm, vmem],
        out_specs=(hbm, vmem, vmem),
        scratch_shapes=[
            pltpu.VMEM((chips, words, here), jnp.int32),
            pltpu.VMEM((inputs, units), BF16),
            pltpu.VMEM((units, inputs), BF16),
            pltpu.VMEM((units, LANES), F32),
            pltpu.VMEM((inputs, block), BF16),
            pltpu.VMEM((pair, samples), BF16),
            pltpu.VMEM((units, samples), BF16),
            pltpu.VMEM((rows, units), F32),
            pltpu.VMEM((rows, units), F32),
            pltpu.VMEM((pair + PAD, units), BF16),
            pltpu.VMEM((pair + PAD, samples), BF16),
            pltpu.VMEM((parts, pair + PAD, part), F32),
            pltpu.VMEM((parts, pair + PAD, part), F32),
            pltpu.VMEM((rows, units), F32),
            pltpu.VMEM((2, peers, 1, samples), F32),
            pltpu.VMEM((2, groups * shards, 1, LANES), F32),
            pltpu.VMEM((2, 2, 8, LANES), F32),
            dma((2 + units // min(UNITS, units),)),
            dma,
            dma((chips, here // block)),
            dma((2,)),
            dma,
            dma((parts,)),
            dma,
            dma((2,)),
            dma((2,)),
            dma((2,)),
            dma((2,)),
            dma((2, 2)),
            pltpu.SemaphoreType.REGULAR,
        ],
        compiler_params=pltpu.CompilerParams(
            collective_id=0, has_side_effects=True, vmem_limit_bytes=67043328
        ),
    )(spins_packed, weight, bias_row, force_w, force_row)
    update_w, update_b = pl.pallas_call(
        finish,
        out_shape=(wide, thin),
        in_specs=[vmem] * 5,
        out_specs=(vmem, vmem),
    )(force_w, force_row, res, res_b, coef)
    return update_w, update_b.reshape(-1)


def solution(mesh):
    placed = (P(None, "smp"), P(None, "grp"), P("grp"), P("smp", "grp"), P("grp"))
    return jax.shard_map(
        functools.partial(body, mesh.shape["grp"], mesh.shape["smp"]),
        mesh=mesh, in_specs=placed, out_specs=(P("smp", "grp"), P("grp")), check_vma=False,
    )
```

time: 70.9 us -> 63.7 us (0.90)
  Pallas kernels: 66.4 us -> 62.8 us
  local copies, waits for them, and re-layouts: 3.59 us -> 0 us
    pallas_call x1 -> x2, Pallas kernels: 66.4 us -> 62.8 us  [the longest x1 60 us: body(): pl.pallas_call(functools.partial(kernel, groups, shards, pieces), out_sha...]
    unnamed x2 -> x0, local copies, waits for them, and re-layouts: 3.59 us -> none
where the time goes in v2:
time: 63.7 us; the launch traced here: 63.4 us
  Pallas kernels  62.8 us (99%)
  between operations  0.64 us (1%)
    pallas_call x1, Pallas kernels, body(): pl.pallas_call(functools.partial(kernel, groups, shards, pieces), out_sha...  60 us
    pallas_call x1, Pallas kernels, body(): pl.pallas_call(finish, out_shape=(wide, thin), in_specs=[vmem] * 5, out_s...  2.84 us

profile of v2, /device:TPU:0, one launch (start us, length us, event | category | flops | bytes accessed | tf_op | source)
XLA Modules:
  0.0 63.4 jit_solution(5729330382507717457)
XLA Ops:
  0.6 60.0 %shard_map.68 = (f32[128,2048]{1,0:T(8,128)}, f32[1,2048]{1,0:T(1,128)}, f32[1,128]{1,0:T(1,128)}) custom-call(s32[32,1024]{1,0:T(8,128)} %packed_hbm.1, bf16[1024,2048]{1,0:T(8,128)(2,1)} %weight_hbm.1, f32[1,2048]{1,0:T(1,128)} %bitcast.5, f32[128,2048]{1,0:T(8,128)} %force_ref.1, f32[1,2048]{1,0:T(1,128)} %bitcast.3), custom_call_target="tpu_custom_call" | custom-call | tf_op jit(solution)/shard_map/pallas_call | solution.py:371
  60.6 2.8 %shard_map.69 = (f32[128,2048]{1,0:T(8,128)}, f32[1,2048]{1,0:T(1,128)}) custom-call(f32[128,2048]{1,0:T(8,128)} %force_ref.1, f32[1,2048]{1,0:T(1,128)} %bitcast.4, f32[128,2048]{1,0:T(8,128)} %get-tuple-element.7.res_ref, f32[1,2048]{1,0:T(1,128)} %get-tuple-element.8.res_b_ref, f32[1,128]{1,0:T(1,128)} %get-tuple-element.9.coef_ref), custom_call_target="tpu_custom_call" | custom-call | tf_op jit(solution)/shard_map/pallas_call | solution.py:412

commit v3 on v2

--- a/solution.py
+++ b/solution.py
@@ -12,10 +12,10 @@
 diag_shift = 0.01
 LANES = 128
 PAD = 16
-BLOCK = 512
+BLOCK = 1024
 UNITS = 512
-PART = 256
-LAG = 2
+PART = 512
+LAG = 1
 FEW = 32
 
 
@@ -169,7 +169,18 @@
     def anyone(step):
         return lax.rem(grp + step // shards, groups), lax.rem(smp + lax.rem(step, shards), shards)
 
+    def meet():
+        pl.semaphore_wait(barrier, groups + shards - 2)
+        for step in range(1, chips):
+            for at in range(tiles):
+                packed_copy(chip, chip_of(step), at).start()
+        loads[1].wait()
+        force_copy.start()
+        for step in range(1, shards):
+            pl.semaphore_signal(ready, device_id={"smp": lax.rem(smp + step, shards)}, device_id_type=MESH)
+
     width = min(256, unit_block)
+    ahead_units = (units + 1) // 2 if tiles == 1 else units
     loads[0].wait()
     unpack(chip, 0, columns(chip, 0))
     for unit in range(0, units, unit_block):
@@ -178,14 +189,8 @@
             weight_t[start : start + width, :] = weight_in[:, start : start + width].T
             bias_t[start : start + width, :] = jnp.broadcast_to(bias_ref[:, start : start + width], (LANES, width)).T
         activate(unit, columns(chip, 0))
-    loads[1].wait()
-    pl.semaphore_wait(barrier, groups + shards - 2)
-    for step in range(1, chips):
-        for at in range(tiles):
-            packed_copy(chip, chip_of(step), at).start()
-    force_copy.start()
-    for step in range(1, shards):
-        pl.semaphore_signal(ready, device_id={"smp": lax.rem(smp + step, shards)}, device_id_type=MESH)
+        if unit < ahead_units <= unit + unit_block:
+            meet()
     for at in range(1, tiles):
         unpack(chip, at, columns(chip, at))
         for unit in range(0, units, unit_block):
@@ -260,7 +265,6 @@
     value0, norm0, _, sum0 = reduce_values(0, force_dot, jnp.zeros((1, 1), F32))
     centred = value0 - sum0 / count
     square_start(0, centred)
-
     weights = centred.astype(BF16)
     for at in range(0, samples, block):
         scaled[:pair, at : at + block] = spins[:, at : at + block] * weights[:, at : at + block]
@@ -273,7 +277,7 @@
         )
 
     def image_part(at):
-        these = pl.ds(pl.multiple_of(at * part, part), part)
+        these = pl.ds(at * part, part)
         image[at] = lax.dot_general(
             scaled[...], hidden[these, :], (((1,), (1,)), ((), ())), preferred_element_type=F32
         )
@@ -282,12 +286,12 @@
     scale = 1.0 / count
 
     def store(at):
-        cols = pl.ds(pl.multiple_of(at * part, part), part)
+        cols = pl.ds(at * part, part)
         return pltpu.make_async_copy(residual.at[:, cols], res_hbm.at[:, cols], store_sem)
 
     def residual_part(at, step0, norms):
         first, second = norms
-        these = pl.ds(pl.multiple_of(at * part, part), part)
+        these = pl.ds(at * part, part)
         image_copy(at).wait_recv()
 
         def next_residual(which, force):
@@ -315,14 +319,14 @@
     all_packed().wait_send()
 
     def next_part(at, norms):
-        norms = residual_part(at - ahead, step0, norms)
         image_part(at)
-        return norms
-
-    none = jnp.zeros((1, part), F32)
-    norms = lax.fori_loop(ahead, parts, next_part, (none, none))
-    norms = lax.fori_loop(parts - ahead, parts, lambda at, norms: residual_part(at, step0, norms), norms)
-
+        return residual_part(at - ahead, step0, norms)
+
+    norms = jnp.zeros((1, part), F32), jnp.zeros((1, part), F32)
+    for at in range(ahead, parts):
+        norms = next_part(at, norms)
+    for at in range(parts - ahead, parts):
+        norms = residual_part(at, step0, norms)
     def second_values(at, carry):
         cols = pl.ds(pl.multiple_of(at * block, block), block)
         values[1, slot, :, cols] = values_of(cols)

time: 63.7 us -> 61.2 us (0.961)
  Pallas kernels: 62.8 us -> 60.3 us
    pallas_call x1, Pallas kernels: 60 us -> 57.5 us  [body(): pl.pallas_call(functools.partial(kernel, groups, shards, pieces), out_sha...]
where the time goes in v3:
time: 61.2 us; the launch traced here: 61 us
  Pallas kernels  60.3 us (99%)
  between operations  0.64 us (1%)
    pallas_call x1, Pallas kernels, body(): pl.pallas_call(functools.partial(kernel, groups, shards, pieces), out_sha...  57.5 us
    pallas_call x1, Pallas kernels, body(): pl.pallas_call(finish, out_shape=(wide, thin), in_specs=[vmem] * 5, out_s...  2.84 us

profile of v3, /device:TPU:0, one launch (start us, length us, event | category | flops | bytes accessed | tf_op | source)
XLA Modules:
  0.0 61.0 jit_solution(3578982762564677413)
XLA Ops:
  0.6 57.5 %shard_map.68 = (f32[128,2048]{1,0:T(8,128)}, f32[1,2048]{1,0:T(1,128)}, f32[1,128]{1,0:T(1,128)}) custom-call(s32[32,1024]{1,0:T(8,128)} %packed_hbm.1, bf16[1024,2048]{1,0:T(8,128)(2,1)} %weight_hbm.1, f32[1,2048]{1,0:T(1,128)} %bitcast.5, f32[128,2048]{1,0:T(8,128)} %force_ref.1, f32[1,2048]{1,0:T(1,128)} %bitcast.3), custom_call_target="tpu_custom_call" | custom-call | tf_op jit(solution)/shard_map/pallas_call | solution.py:375
  58.1 2.8 %shard_map.69 = (f32[128,2048]{1,0:T(8,128)}, f32[1,2048]{1,0:T(1,128)}) custom-call(f32[128,2048]{1,0:T(8,128)} %force_ref.1, f32[1,2048]{1,0:T(1,128)} %bitcast.4, f32[128,2048]{1,0:T(8,128)} %get-tuple-element.7.res_ref, f32[1,2048]{1,0:T(1,128)} %get-tuple-element.8.res_b_ref, f32[1,128]{1,0:T(1,128)} %get-tuple-element.9.coef_ref), custom_call_target="tpu_custom_call" | custom-call | tf_op jit(solution)/shard_map/pallas_call | solution.py:416

commit v4 on v3

--- a/solution.py
+++ b/solution.py
@@ -37,7 +37,7 @@
     res_hbm, res_b_ref, coef_ref,
     packed, weight_in, weight_t, bias_t, tile, spins, hidden, force_own, force_other, lhs, scaled,
     image, image_other, residual, values, extras, squares,
-    load_sem, packed_send, packed_recv, force_sem, image_send, image_recv, store_sem,
+    load_sem, packed_send, packed_recv, spread_send, spread_recv, share_send, share_recv, force_sem, image_send, image_recv, store_sem,
     value_send, value_recv, extra_send, extra_recv, square_sem, ready,
 ):
     grp, smp = lax.axis_index("grp"), lax.axis_index("smp")
@@ -91,6 +91,26 @@
             device_id={"smp": 2 * target + core}, device_id_type=MESH,
         )
 
+    slice_ = here // groups
+
+    def quarter_copy(source, send, recv, device):
+        where = packed.at[source, :, pl.ds(pl.multiple_of(grp * slice_, slice_), slice_)]
+        return pltpu.make_async_remote_copy(
+            where, where, send, recv.at[source], device_id=device, device_id_type=MESH
+        )
+
+    def spread(source, target):
+        return quarter_copy(source, spread_send, spread_recv, {"smp": 2 * target + core})
+
+    def share(source, step):
+        return quarter_copy(source, share_send, share_recv, {"grp": lax.rem(grp + step, groups)})
+
+    def all_of(sources, columns_of, send, recv):
+        where = packed.at[sources, :, pl.ds(0, columns_of)]
+        return pltpu.make_async_remote_copy(
+            where, where, send, recv, device_id={"smp": sibling}, device_id_type=MESH
+        )
+
     force_copy = pltpu.make_async_remote_copy(
         force_own, force_other, force_sem.at[0], force_sem.at[1],
         device_id={"smp": sibling}, device_id_type=MESH,
@@ -159,21 +179,15 @@
             device_id={"smp": sibling}, device_id_type=MESH,
         )
 
-    def all_packed():
-        where = packed.at[pl.ds(0, chips - 1)]
-        return pltpu.make_async_remote_copy(
-            where, where, packed_send, packed_recv.at[chip, 0],
-            device_id={"smp": sibling}, device_id_type=MESH,
-        )
-
     def anyone(step):
         return lax.rem(grp + step // shards, groups), lax.rem(smp + lax.rem(step, shards), shards)
 
     def meet():
         pl.semaphore_wait(barrier, groups + shards - 2)
-        for step in range(1, chips):
-            for at in range(tiles):
-                packed_copy(chip, chip_of(step), at).start()
+        for step in range(2, chips):
+            spread(chip, chip_of(step)).start()
+        for at in range(tiles):
+            packed_copy(chip, chip_of(1), at).start()
         loads[1].wait()
         force_copy.start()
         for step in range(1, shards):
@@ -204,6 +218,10 @@
     lhs[own_rows(1 - core), :] = force_other[...].astype(BF16)
     for at in range(tiles):
         values[0, slot, :, columns(chip, at)] = values_of(columns(chip, at))
+    for step in range(2, chips):
+        spread(chip_of(step), chip).wait_recv()
+        for peer in range(1, groups):
+            share(chip_of(step), peer).start()
     pl.semaphore_wait(ready, shards - 1)
     if pieces == turns:
         for at in range(tiles):
@@ -212,7 +230,15 @@
     def remote_tile(turn_at, carry):
         at_chip, in_chip = chip_of(turn_at // tiles), lax.rem(turn_at, tiles)
         cols = columns(at_chip, in_chip)
-        packed_copy(at_chip, chip, in_chip).wait_recv()
+
+        @pl.when(turn_at < 2 * tiles)
+        def _():
+            packed_copy(at_chip, chip, in_chip).wait_recv()
+
+        @pl.when((turn_at >= 2 * tiles) & (in_chip == 0))
+        def _():
+            all_of(at_chip, (groups - 1) * slice_, share_send, share_recv.at[at_chip]).wait_recv()
+
         unpack(at_chip, in_chip, cols)
         for unit in range(0, units, unit_block):
             activate(unit, cols)
@@ -316,7 +342,10 @@
     each(0, ahead, image_part)
     step0 = norm0 / (square_total(0) + diag_shift * norm0)
     drain(0)
-    all_packed().wait_send()
+    far = pl.ds(0, chips - 2)
+    all_of(chip, here, packed_send, packed_recv.at[chip, 0]).wait_send()
+    all_of(far, slice_, spread_send, spread_recv.at[chip]).wait_send()
+    all_of(far, (groups - 1) * slice_, share_send, share_recv.at[chip]).wait_send()
 
     def next_part(at, norms):
         image_part(at)
@@ -398,6 +427,10 @@
             dma((2 + units // min(UNITS, units),)),
             dma,
             dma((chips, here // block)),
+            dma,
+            dma((chips,)),
+            dma,
+            dma((chips,)),
             dma((2,)),
             dma,
             dma((parts,)),

time: 61.2 us -> 60 us (0.980)
  Pallas kernels: 60.3 us -> 59.1 us
    pallas_call x1, Pallas kernels: 57.5 us -> 56.3 us  [body(): pl.pallas_call(functools.partial(kernel, groups, shards, pieces), out_sha...]
where the time goes in v4:
time: 60 us; the launch traced here: 59.7 us
  Pallas kernels  59.1 us (98%)
  between operations  0.64 us (1%)
    pallas_call x1, Pallas kernels, body(): pl.pallas_call(functools.partial(kernel, groups, shards, pieces), out_sha...  56.3 us
    pallas_call x1, Pallas kernels, body(): pl.pallas_call(finish, out_shape=(wide, thin), in_specs=[vmem] * 5, out_s...  2.84 us

profile of v4, /device:TPU:0, one launch (start us, length us, event | category | flops | bytes accessed | tf_op | source)
XLA Modules:
  0.0 59.7 jit_solution(7873882289275998669)
XLA Ops:
  0.6 56.3 %shard_map.68 = (f32[128,2048]{1,0:T(8,128)}, f32[1,2048]{1,0:T(1,128)}, f32[1,128]{1,0:T(1,128)}) custom-call(s32[32,1024]{1,0:T(8,128)} %packed_hbm.1, bf16[1024,2048]{1,0:T(8,128)(2,1)} %weight_hbm.1, f32[1,2048]{1,0:T(1,128)} %bitcast.5, f32[128,2048]{1,0:T(8,128)} %force_ref.1, f32[1,2048]{1,0:T(1,128)} %bitcast.3), custom_call_target="tpu_custom_call" | custom-call | tf_op jit(solution)/shard_map/pallas_call | solution.py:404
  56.9 2.8 %shard_map.69 = (f32[128,2048]{1,0:T(8,128)}, f32[1,2048]{1,0:T(1,128)}) custom-call(f32[128,2048]{1,0:T(8,128)} %force_ref.1, f32[1,2048]{1,0:T(1,128)} %bitcast.4, f32[128,2048]{1,0:T(8,128)} %get-tuple-element.7.res_ref, f32[1,2048]{1,0:T(1,128)} %get-tuple-element.8.res_b_ref, f32[1,128]{1,0:T(1,128)} %get-tuple-element.9.coef_ref), custom_call_target="tpu_custom_call" | custom-call | tf_op jit(solution)/shard_map/pallas_call | solution.py:449
